TPU v7x, 32 devices: a whole 2x2x4 slice. The times are simulated.
32 devices in a mesh: tiles: 2 (over x), slab: 16 (over z, y, core).
Axes of the slice: x: 2, y: 2, z: 4, core: 2. Of those that a mesh axis runs over, the one named last changes fastest.
Arguments:
- transmission: float32 [8192, 4096], P(('tiles', 'slab')), parts along dimension 0, may hold values from -6 to 6
- kernel_spectra: float32 [12, 2, 256, 256], replicated, may hold values from -6 to 6
Outputs:
- resist_image: float32 [8192, 256], P(('tiles', 'slab')), parts along dimension 0
There are 2 independent parts, one for each index of `tiles`. A program takes and returns all parts, laid end to end along the dimension named above; an argument that names none is the same for every part. Nothing has to cross between parts.
All inputs are finite; a program needn't handle non-finite values.
Results may differ from a plain program's by a relative error of at most 0.0001.
Values sent between devices are 32-bit elements; how exact they have to be, the bound alone decides.
A program may use at most 128 MiB of HBM per device.

v0:
```python
import math

import jax
import jax.numpy as jnp
from jax import lax
from jax.sharding import PartitionSpec as P

COLS = 256


binomial = (0.0625, 0.25, 0.375, 0.25, 0.0625)


def extended(x, sides, width):
    for axis, dim in sides:
        size, length = (lax.axis_size(axis), x.shape[dim])
        up = [(i, (i + 1) % size) for i in range(size)]
        down = [(j, i) for i, j in up]
        last = lax.slice_in_dim(x, length - width, length, axis=dim)
        leading = lax.slice_in_dim(x, 0, width, axis=dim)
        before = lax.ppermute(last, axis, up)
        after = lax.ppermute(leading, axis, down)
        x = jnp.concatenate([before, x, after], axis=dim)
    return x


def phase_tables(positions, tile_side, band_size):
    frequency = jnp.arange(band_size, dtype=jnp.int32) - band_size // 2
    residue = jnp.mod(positions[:, None] * frequency[None, :], tile_side)
    angles = residue.astype(jnp.float32) * (2.0 * math.pi / tile_side)
    return (jnp.cos(angles), jnp.sin(angles))


def product(left, right):
    return jnp.dot(left, right, precision=lax.Precision.HIGHEST, preferred_element_type=jnp.float32)


def contract_first(left, right):
    return lax.dot_general(
        left,
        right,
        (((0,), (0,)), ((), ())),
        precision=lax.Precision.HIGHEST,
        preferred_element_type=jnp.float32,
    )


def contract_last(left, right):
    return lax.dot_general(
        left,
        right,
        (((1,), (1,)), ((), ())),
        precision=lax.Precision.HIGHEST,
        preferred_element_type=jnp.float32,
    )


def kernel_intensity(
    row_cosine,
    row_sine,
    cosine_table,
    sine_table,
    spectrum_real,
    spectrum_imag,
    kernel_spectra,
    norm_factor,
):
    half_rows = row_cosine.shape[0]

    def accumulate(running, kernel):
        prod_real = (kernel[0] * spectrum_real - kernel[1] * spectrum_imag) * norm_factor
        prod_imag = (kernel[0] * spectrum_imag + kernel[1] * spectrum_real) * norm_factor
        left_real = product(row_cosine, prod_real) - product(row_sine, prod_imag)
        left_imag = product(row_cosine, prod_imag) + product(row_sine, prod_real)
        stacked = jnp.concatenate([left_real, left_imag], 0)
        with_cosine = contract_last(stacked, cosine_table)
        with_sine = contract_last(stacked, sine_table)
        field_real = with_cosine[:half_rows] - with_sine[half_rows:]
        field_imag = with_sine[:half_rows] + with_cosine[half_rows:]
        return (running + field_real * field_real + field_imag * field_imag, None)

    start = jnp.zeros((half_rows, cosine_table.shape[0]), jnp.float32)
    running, unused = lax.scan(accumulate, start, kernel_spectra)
    return running / kernel_spectra.shape[0]


def local(transmission, kernel_spectra):
    row_count = transmission.shape[0]
    tile_side = transmission.shape[1]
    band_size = kernel_spectra.shape[2]
    offset = lax.axis_index("slab") * row_count
    cosine_table, sine_table = phase_tables(
        jnp.arange(tile_side, dtype=jnp.int32), tile_side, band_size
    )
    window_positions = jnp.mod(jnp.arange(COLS + 4, dtype=jnp.int32) - 2, tile_side)
    out_cosine, out_sine = phase_tables(window_positions, tile_side, band_size)
    own_cosine = lax.dynamic_slice_in_dim(cosine_table, offset, row_count, 0)
    own_sine = lax.dynamic_slice_in_dim(sine_table, offset, row_count, 0)
    column_real = product(transmission, cosine_table)
    column_imag = -product(transmission, sine_table)
    spectrum_real = contract_first(own_cosine, column_real) + contract_first(own_sine, column_imag)
    spectrum_imag = contract_first(own_cosine, column_imag) - contract_first(own_sine, column_real)
    spectrum_real, spectrum_imag = lax.psum((spectrum_real, spectrum_imag), "slab")
    norm_factor = 1.0 / (tile_side * band_size)
    intensity = kernel_intensity(
        own_cosine,
        own_sine,
        out_cosine,
        out_sine,
        spectrum_real,
        spectrum_imag,
        kernel_spectra,
        norm_factor,
    )
    padded = extended(intensity, (("slab", 0),), 2)
    row_blurred = jnp.zeros_like(intensity)
    for position, weight in enumerate(binomial):
        row_blurred = row_blurred + weight * padded[position : position + row_count]
    resist_image = jnp.zeros((row_count, COLS), jnp.float32)
    for position, weight in enumerate(binomial):
        resist_image = resist_image + weight * row_blurred[:, position : position + COLS]
    return resist_image


def solution(mesh):
    return jax.shard_map(
        local,
        mesh=mesh,
        in_specs=(P(("tiles", "slab"), None), P()),
        out_specs=P(("tiles", "slab"), None),
        check_vma=False,
    )
```

profile of v0, /device:TPU:0, one launch (start us, length us, event | category | flops | bytes accessed | tf_op | source)
XLA Modules:
  0.0 258.2 jit_solution(3038581356654749659)
XLA Ops:
  6.5 17.9 %fusion.35 = (f32[4096,256]{1,0:T(8,128)}, f32[4096,256]{1,0:T(8,128)}) fusion(s32[256]{0:T(256)S(1)} %iota_add_fusion), kind=kLoop, calls=%fused_computation.48 | loop fusion | flops 14680064 | bytes 8389632 | tf_op jit(solution)/shard_map/sin | solution.py:31
  24.5 22.3 %fusion.41 = f32[256,256]{1,0:T(8,128)S(1)} fusion(f32[256,4096]{1,0:T(8,128)S(1)} %copy-done, s32[256]{0:T(256)S(1)} %iota_add_fusion), kind=kOutput, calls=%fused_computation.54 | convolution fusion | flops 3235971072 | bytes 4457472 | tf_op jit(solution)/shard_map/dot_general | solution.py:35
  46.8 22.6 %fusion.37 = f32[256,256]{1,0:T(8,128)S(1)} fusion(f32[256,4096]{1,0:T(8,128)S(1)} %copy-done, s32[256]{0:T(256)S(1)} %iota_add_fusion), kind=kOutput, calls=%fused_computation.50 | convolution fusion | flops 3235905536 | bytes 4457472 | tf_op jit(solution)/shard_map/dot_general | solution.py:35
  69.3 1.1 constant_dynamic-slice_fusion
  70.4 0.6 fusion.71
  71.0 0.6 fusion.70
  71.6 1.3 convolution_subtract_fusion.1
  72.9 1.3 convolution_add_fusion.1
  74.2 93.5 %all-reduce.3.cloned.1.call-done = (f32[256,256]{1,0:T(8,128)}, f32[256,256]{1,0:T(8,128)}) async-done(((f32[256,256]{1,0:T(8,128)}, f32[256,256]{1,0:T(8,128)}), (f32[256,256]{1,0:T(8,128)}, f32[256,256]{1,0:T(8,128)})) %all-reduce.3.cloned.1.call-update) | async-done | bytes 524304 | tf_op jit(solution)/shard_map/psum | solution.py:103
  167.8 76.3 %while.13 = (s32[]{:T(128)}, f32[256,260]{0,1:T(8,128)S(1)}, f32[12,2,256,256]{3,2,1,0:T(8,128)}, f32[256,256]{1,0:T(8,128)}, f32[256,256]{1,0:T(8,128)}, /*inde...) while((s32[]{:T(128)}, f32[256,260]{0,1:T(8,128)S(1)}, ...), condition=%wide.region_3.4_spmd.clone.clone.clone, body=%wide.region_2.3_spmd.clone.clone.clone.sunk | while | flops 1626442752 | bytes 8958131 | solution.py:83
  167.8 1.3 subtract_multiply_fusion.2
  170.3 0.4 fusion.118
  170.7 1.6 fusion.122
  172.3 1.6 fusion.121
  174.1 1.3 subtract_multiply_fusion.2
  176.6 0.4 fusion.118
  177.0 1.6 fusion.122
  178.7 1.6 fusion.121
  180.5 1.3 subtract_multiply_fusion.2
  182.2 0.4 fusion.120
  183.0 0.4 fusion.118
  183.4 1.6 fusion.122
  185.0 1.6 fusion.121
  186.9 1.3 subtract_multiply_fusion.2
  188.5 0.4 fusion.120
  189.3 0.4 fusion.118
  189.8 1.6 fusion.122
  191.4 1.6 fusion.121
  193.2 1.3 subtract_multiply_fusion.2
  195.7 0.4 fusion.118
  196.1 1.6 fusion.122
  197.8 1.6 fusion.121
  199.6 1.3 subtract_multiply_fusion.2
  202.1 0.4 fusion.118
  202.5 1.6 fusion.122
  204.1 1.6 fusion.121
  205.9 1.3 subtract_multiply_fusion.2
  208.4 0.4 fusion.118
  208.8 1.6 fusion.122
  210.5 1.6 fusion.121
  212.3 1.3 subtract_multiply_fusion.2
  214.8 0.4 fusion.118
  215.2 1.6 fusion.122
  216.8 1.6 fusion.121
  218.7 1.3 subtract_multiply_fusion.2
  221.1 0.4 fusion.118
  221.5 1.6 fusion.122
  223.2 1.6 fusion.121
  225.0 1.3 subtract_multiply_fusion.2
  227.5 0.4 fusion.118
  227.9 1.6 fusion.122
  229.5 1.6 fusion.121
  231.4 1.3 subtract_multiply_fusion.2
  233.9 0.4 fusion.118
  234.3 1.6 fusion.122
  235.9 1.6 fusion.121
  237.7 1.3 subtract_multiply_fusion.2
  240.2 0.4 fusion.118
  240.6 1.6 fusion.122
  242.3 1.6 fusion.121
  244.3 0.5 collective-permute-start
  244.8 4.0 %collective-permute-start.1 = (f32[2,260]{1,0:T(2,128)S(1)}, f32[2,260]{1,0:T(2,128)S(1)}, u32[]{:S(2)}, u32[]{:S(2)}) collective-permute-start(f32[2,260]{1,0:T(2,128)S(1)} %get-tuple-element.170), channel_id=1, source_target_pairs={{1,0},{2,1},{3,2},{4,3},{5,4},{6,5},{7,6},{8,7},{9,8},{10,9},{11,1... | collective-permute-start | bytes 6248 | tf_op jit(solution)/shard_map/ppermute | solution.py:22
  248.8 1.3 collective-permute-done
  250.4 1.0 fusion.54
  (58 shorter events, 16.0 us)
Async XLA Ops:
  6.5 161.3 %all-reduce.3.cloned.1.call-start = ((), (), s32[]{:S(2)}) async-start(), calls=%async_computation | async-start | bytes 1048576 | tf_op jit(solution)/shard_map/psum | solution.py:103
  6.5 17.9 %copy-start = (f32[256,4096]{1,0:T(8,128)S(1)}, f32[256,4096]{1,0:T(8,128)}, u32[]{:S(2)}) copy-start(f32[256,4096]{1,0:T(8,128)} %param.4) | copy-start | bytes 12582916
  244.3 5.8 %collective-permute-start = (f32[2,260]{1,0:T(2,128)S(1)}, f32[2,260]{1,0:T(2,128)S(1)}, u32[]{:S(2)}, u32[]{:S(2)}) collective-permute-start(f32[2,260]{1,0:T(2,128)S(1)} %get-tuple-element.169), channel_id=1, source_target_pairs={{0,1},{1,2},{2,3},{3,4},{4,5},{5,6},{6,7},{7,8},{8,9},{9,10},{10,1... | collective-permute-start | bytes 6248 | tf_op jit(solution)/shard_map/ppermute | solution.py:21
  244.8 5.3 %collective-permute-start.1 = (f32[2,260]{1,0:T(2,128)S(1)}, f32[2,260]{1,0:T(2,128)S(1)}, u32[]{:S(2)}, u32[]{:S(2)}) collective-permute-start(f32[2,260]{1,0:T(2,128)S(1)} %get-tuple-element.170), channel_id=1, source_target_pairs={{1,0},{2,1},{3,2},{4,3},{5,4},{6,5},{7,6},{8,7},{9,8},{10,9},{11,1... | collective-permute-start | bytes 6248 | tf_op jit(solution)/shard_map/ppermute | solution.py:22
Sparse Core Ops, SparseCore 0:
  74.3 93.4 all-reduce.2
where the time goes:
time: 259 us; the launch traced here: 258 us
  matrix products  107 us (41%)
  waiting for transfers between devices  94.9 us (37%)
  other arithmetic  36.4 us (14%)
  between operations  13.5 us (5%)
  starting transfers between devices  4.5 us (2%)
    psum x1, waiting for transfers between devices, local(): lax.psum((spectrum_real, spectrum_imag), 'slab')  93.5 us
    dot_general x50, matrix products, product(): jnp.dot(left, right, precision=lax.Precision.HIGHEST, preferred_element_t...  64 us
    dot_general x24, matrix products, contract_last(): lax.dot_general(left, right, (((1,), (1,)), ((), ())), precision=lax.Prec...  39.1 us
    sin x1, other arithmetic, phase_tables(): return (jnp.cos(angles), jnp.sin(angles))  17.9 us
    mul x12, other arithmetic, accumulate(): (kernel[0] * spectrum_real - kernel[1] * spectrum_imag) * norm_factor  15.2 us
  transfers between devices with their start and end apart: 3, of which 2 were waited for; matrix products, arithmetic and copies ran while one was open for 0% of the time, Pallas kernels for 0%

commit v1 on v0

v1 whole, which is shorter than its diff:
```python
import functools
import math

import jax
import jax.numpy as jnp
import numpy as np
from jax import lax
from jax.experimental import pallas as pl
from jax.experimental.pallas import tpu as pltpu
from jax.sharding import PartitionSpec as P

COLS = 256
LANES = 128
CHUNK = 512
binomial = (0.0625, 0.25, 0.375, 0.25, 0.0625)
MESH = pl.DeviceIdType.MESH


def halves_of(table):
    high = np.asarray(table, np.float32).astype(jnp.bfloat16)
    low = (np.asarray(table, np.float64) - high.astype(np.float64)).astype(jnp.bfloat16)
    return high, low


def angle(positions, frequency, side):
    residue = np.mod(np.outer(positions, frequency), side)
    return residue.astype(np.float64) * (2.0 * math.pi / side)


@functools.lru_cache(maxsize=None)
def tables(slabs, rows, side, band, chunk):
    frequency = np.arange(band) - band // 2
    even, odd = frequency[0::2], frequency[1::2]
    y = np.arange(chunk)
    column = np.concatenate(
        [f(angle(y, g, side)) for g in (even, odd) for f in (np.cos, np.sin)], axis=1
    )
    both = np.concatenate([even, odd])
    starts = np.arange(side // 2 // chunk) * chunk
    turn = angle(starts, both, side)
    twiddle = np.stack([np.cos(turn), np.sin(turn)], axis=1).astype(np.float32)
    order = (both[:, None] == frequency[None, :]).astype(jnp.bfloat16)
    x = angle(np.arange(rows), frequency, side).T
    row = np.concatenate([np.cos(x), np.sin(x)], axis=0)
    lanes = -(-slabs // LANES) * LANES
    first = angle(np.arange(lanes) * rows, frequency, side).T
    phase = np.stack([np.cos(first), np.sin(first)]).astype(np.float32)
    total = 2 * band
    stride = side // total
    s = angle(np.arange(0, rows, stride), frequency, side)
    c, d = np.cos(s), np.sin(s)
    sample = np.concatenate(
        [np.concatenate([c, -d], 1), np.concatenate([d, c], 1)], axis=0
    )
    wide = -(-(COLS + 4) // LANES) * LANES
    q = angle(np.arange(wide) - 2, frequency, side).T
    window = np.concatenate([np.cos(q), np.sin(q)], axis=1)
    g = np.arange(-(band - 1), band)
    gain = sum(w * np.cos(angle([u - 2], g, side))[0] for u, w in enumerate(binomial)) / total
    shift = np.arange(side)
    kernel = np.cos(angle(shift, g, side)) @ gain
    index = np.mod(np.arange(rows)[:, None] - stride * np.arange(total)[None, :], side)
    spread = kernel[index]
    return dict(
        column=np.stack(halves_of(column)),
        twiddle=twiddle,
        order=order,
        row=np.stack(halves_of(row)),
        phase=phase,
        sample=np.concatenate(halves_of(sample), axis=0),
        window=np.stack(halves_of(window)),
        spread=np.stack(halves_of(spread)),
    )


NAMES = ("column", "twiddle", "order", "row", "phase", "sample", "window", "spread")


def split(x):
    high = x.astype(jnp.bfloat16)
    return high, (x - high.astype(jnp.float32)).astype(jnp.bfloat16)


def dot(a, b):
    return jnp.dot(a, b, preferred_element_type=jnp.float32)


def dot3(a, b):
    return dot(a[0], b[0]) + dot(a[0], b[1]) + dot(a[1], b[0])


def body(slabs, chunk, t_hbm, k_hbm, *refs):
    count = len(NAMES)
    hbm = dict(zip(NAMES, refs[:count]))
    out = refs[count]
    scratch = refs[count + 1 :]
    t_ref, k_ref = scratch[:2]
    tab = dict(zip(NAMES, scratch[2 : 2 + count]))
    (acc, sbuf, rbuf, fbuf, spec, lbuf, ibuf, load_sem, t_sem, ssem, rsem) = scratch[2 + count :]
    me = lax.axis_index("slab")
    rows, side = t_ref.shape
    kernels, _, band, _ = k_ref.shape
    half = side // 2
    steps = half // chunk
    part = sbuf.shape[0] // slabs
    samples = ibuf.shape[1]

    def peer(k):
        return lax.rem(me + k, slabs)

    barrier = pltpu.get_barrier_semaphore()
    for k in range(1, slabs):
        pl.semaphore_signal(barrier, inc=1, device_id={"slab": peer(k)}, device_id_type=MESH)

    loads = {}
    for i, name in enumerate(NAMES):
        loads[name] = pltpu.make_async_copy(hbm[name], tab[name], load_sem.at[i])
    t_loads = []
    for c in range(steps):
        for h in range(2):
            lanes = pl.ds(h * half + c * chunk, chunk)
            t_loads.append(
                pltpu.make_async_copy(
                    t_hbm.at[:, lanes], t_ref.at[:, lanes], t_sem.at[2 * c + h]
                )
            )
    k_load = pltpu.make_async_copy(k_hbm, k_ref, load_sem.at[count])
    t_loads[0].start()
    t_loads[1].start()
    loads["column"].start()
    loads["twiddle"].start()
    for load in t_loads[2:]:
        load.start()
    for name in ("order", "row", "phase"):
        loads[name].start()
    k_load.start()
    for name in ("sample", "window", "spread"):
        loads[name].start()

    for c in range(steps):
        t_loads[2 * c].wait()
        t_loads[2 * c + 1].wait()
        if c == 0:
            loads["column"].wait()
            loads["twiddle"].wait()
        left = t_ref[:, c * chunk : (c + 1) * chunk]
        right = t_ref[:, half + c * chunk : half + (c + 1) * chunk]
        for j, folded in enumerate((left + right, left - right)):
            lanes = slice(j * band, (j + 1) * band)
            table = (tab["column"][0, :, lanes], tab["column"][1, :, lanes])
            got = dot3(split(folded), table)
            cosine, sine = got[:, : band // 2], got[:, band // 2 :]
            near = slice(j * band // 2, (j + 1) * band // 2)
            far = slice(band + j * band // 2, band + (j + 1) * band // 2)
            if c == 0:
                acc[:, near] = cosine
                acc[:, far] = sine
            else:
                tc = tab["twiddle"][c, 0:1, near]
                ts = tab["twiddle"][c, 1:2, near]
                acc[:, near] += cosine * tc - sine * ts
                acc[:, far] += sine * tc + cosine * ts

    loads["order"].wait()
    loads["row"].wait()
    loads["phase"].wait()
    ordered = []
    for lanes in (slice(0, band), slice(band, 2 * band)):
        ordered.append([dot(p, tab["order"][...]).astype(jnp.bfloat16) for p in split(acc[:, lanes])])
    columns = [jnp.concatenate([ordered[0][i], ordered[1][i]], axis=1) for i in range(2)]
    z = dot3((tab["row"][0], tab["row"][1]), columns)
    re = z[:band, :band] - z[band:, band:]
    im = -(z[:band, band:] + z[band:, :band])
    lane = lax.broadcasted_iota(jnp.int32, tab["phase"].shape[1:], 1)
    pc = jnp.sum(jnp.where(lane == me, tab["phase"][0], 0.0), axis=1, keepdims=True)
    ps = jnp.sum(jnp.where(lane == me, tab["phase"][1], 0.0), axis=1, keepdims=True)
    sbuf[:band, :] = re * pc + im * ps
    sbuf[band:, :] = im * pc - re * ps

    pl.semaphore_wait(barrier, slabs - 1)
    sends = []
    for k in range(1, slabs):
        to = peer(k)
        sends.append(
            pltpu.make_async_remote_copy(
                src_ref=sbuf.at[pl.ds(pl.multiple_of(to * part, part), part)],
                dst_ref=rbuf.at[k - 1],
                send_sem=ssem.at[0, k - 1],
                recv_sem=rsem.at[0, k - 1],
                device_id={"slab": to},
                device_id_type=MESH,
            )
        )
        sends[-1].start()
    own = pl.ds(pl.multiple_of(me * part, part), part)
    total = sbuf[own, :]
    for k in range(1, slabs):
        sends[k - 1].wait_recv()
        total = total + rbuf[k - 1]
    fbuf[own, :] = total
    shares = []
    for k in range(1, slabs):
        shares.append(
            pltpu.make_async_remote_copy(
                src_ref=fbuf.at[own],
                dst_ref=fbuf.at[own],
                send_sem=ssem.at[1, k - 1],
                recv_sem=rsem.at[1, k - 1],
                device_id={"slab": peer(k)},
                device_id_type=MESH,
            )
        )
        shares[-1].start()
    for send in sends:
        send.wait_send()
    k_load.wait()
    for name in ("sample", "window", "spread"):
        loads[name].wait()
    for share in shares:
        share.wait_recv()

    norm = 1.0 / (side * band)
    re, im = fbuf[:band, :], fbuf[band:, :]
    spec[:band, :] = (re * pc - im * ps) * norm
    spec[band:, :] = (im * pc + re * ps) * norm

    def one(k, carry):
        sr, si = spec[:band, :], spec[band:, :]
        kr, ki = k_ref[k, 0], k_ref[k, 1]
        rh, rl = split(kr * sr - ki * si)
        ih, il = split(kr * si + ki * sr)
        high = jnp.concatenate([rh, ih], axis=0)
        low = jnp.concatenate([rl, il], axis=0)
        wide = dot(tab["sample"][...], high)
        lbuf[k] = wide[: 2 * samples] + wide[2 * samples :] + dot(tab["sample"][: 2 * samples, :], low)
        return carry

    lax.fori_loop(0, kernels, one, 0)
    left = split(lbuf[...].reshape(kernels * 2 * samples, band))
    field = dot3(left, (tab["window"][0], tab["window"][1]))
    width = field.shape[1] // 2
    field = field.reshape(kernels, 2 * samples, 2 * width)
    fr = field[:, :samples, :width] - field[:, samples:, width:]
    fi = field[:, :samples, width:] + field[:, samples:, :width]
    intensity = jnp.sum(fr * fr + fi * fi, axis=0) * (1.0 / kernels)
    blurred = binomial[0] * intensity
    for v in range(1, 5):
        blurred = blurred + binomial[v] * pltpu.roll(intensity, width - v, 1)
    ibuf[0] = blurred[:, :COLS]

    rings = []
    for k in range(1, slabs):
        rings.append(
            pltpu.make_async_remote_copy(
                src_ref=ibuf.at[0],
                dst_ref=ibuf.at[slabs - k],
                send_sem=ssem.at[2, k - 1],
                recv_sem=rsem.at[2, k - 1],
                device_id={"slab": peer(k)},
                device_id_type=MESH,
            )
        )
        rings[-1].start()
    for share in shares:
        share.wait_send()
    for ring in rings:
        ring.wait_recv()
    gathered = split(ibuf[...].reshape(slabs * samples, COLS))
    out[...] = dot3((tab["spread"][0], tab["spread"][1]), gathered)
    for ring in rings:
        ring.wait_send()


def local(transmission, kernel_spectra):
    slabs = lax.axis_size("slab")
    rows, side = transmission.shape
    kernels, _, band, _ = kernel_spectra.shape
    chunk = min(CHUNK, side // 2)
    consts = tables(slabs, rows, side, band, chunk)
    arrays = [jnp.asarray(consts[name]) for name in NAMES]
    samples = rows * 2 * band // side
    part = 2 * band // slabs
    any_spec = pl.BlockSpec(memory_space=pl.ANY)
    return pl.pallas_call(
        functools.partial(body, slabs, chunk),
        out_shape=jax.ShapeDtypeStruct((rows, COLS), jnp.float32),
        in_specs=[any_spec] * (2 + len(NAMES)),
        out_specs=pl.BlockSpec(memory_space=pltpu.VMEM),
        scratch_shapes=[
            pltpu.VMEM(transmission.shape, jnp.float32),
            pltpu.VMEM(kernel_spectra.shape, jnp.float32),
            *[pltpu.VMEM(a.shape, a.dtype) for a in arrays],
            pltpu.VMEM((rows, 2 * band), jnp.float32),
            pltpu.VMEM((2 * band, band), jnp.float32),
            pltpu.VMEM((slabs - 1, part, band), jnp.float32),
            pltpu.VMEM((2 * band, band), jnp.float32),
            pltpu.VMEM((2 * band, band), jnp.float32),
            pltpu.VMEM((kernels, 2 * samples, band), jnp.float32),
            pltpu.VMEM((slabs, samples, COLS), jnp.float32),
            pltpu.SemaphoreType.DMA((len(NAMES) + 1,)),
            pltpu.SemaphoreType.DMA((2 * (side // 2 // chunk),)),
            pltpu.SemaphoreType.DMA((3, slabs - 1)),
            pltpu.SemaphoreType.DMA((3, slabs - 1)),
        ],
        compiler_params=pltpu.CompilerParams(
            collective_id=0, has_side_effects=True, vmem_limit_bytes=48 * 1024 * 1024
        ),
    )(transmission, kernel_spectra, *arrays)


def solution(mesh):
    return jax.shard_map(
        local,
        mesh=mesh,
        in_specs=(P(("tiles", "slab"), None), P()),
        out_specs=P(("tiles", "slab"), None),
        check_vma=False,
    )
```

time: 259 us -> 57.6 us (0.22)
  the two profiles are of different devices: /device:TPU:0 before, /device:TPU:13 now
where the time goes in v1:
time: 57.6 us; the launch traced here: 57.2 us
  Pallas kernels  48.6 us (84%)
  local copies, waits for them, and re-layouts  8.6 us (15%)
    pallas_call x1, Pallas kernels, local(): pl.pallas_call(functools.partial(body, slabs, chunk), out_shape=jax.Shape...  48.6 us
    unnamed x17, local copies, waits for them, and re-layouts  8.6 us

profile of v1, /device:TPU:13, one launch (start us, length us, event | category | flops | bytes accessed | tf_op | source)
XLA Modules:
  0.0 57.2 jit_solution(12381773203336101432)
XLA Ops:
  0.0 0.0 copy-start
  0.0 1.2 %copy-done = bf16[2,512,512]{2,1,0:T(8,128)(2,1)S(1)} copy-done((bf16[2,512,512]{2,1,0:T(8,128)(2,1)S(1)}, bf16[2,512,512]{2,1,0:T(8,128)(2,1)}, u32[]{:S(2)}) %copy-start) | copy-done | bytes 1048600
  1.2 0.0 copy-start.1
  1.2 1.1 %copy-done.1 = bf16[2,256,768]{2,1,0:T(8,128)(2,1)S(1)} copy-done((bf16[2,256,768]{2,1,0:T(8,128)(2,1)S(1)}, bf16[2,256,768]{2,1,0:T(8,128)(2,1)}, u32[]{:S(2)}) %copy-start.1) | copy-done | bytes 786456
  2.4 0.0 copy-start.2
  2.4 1.0 %copy-done.2 = bf16[2,256,512]{2,1,0:T(8,128)(2,1)S(1)} copy-done((bf16[2,256,512]{2,1,0:T(8,128)(2,1)S(1)}, bf16[2,256,512]{2,1,0:T(8,128)(2,1)}, u32[]{:S(2)}) %copy-start.2) | copy-done | bytes 524312
  3.4 0.0 copy-start.3
  3.4 1.0 %copy-done.3 = bf16[2,512,256]{2,1,0:T(8,128)(2,1)S(1)} copy-done((bf16[2,512,256]{2,1,0:T(8,128)(2,1)S(1)}, bf16[2,512,256]{2,1,0:T(8,128)(2,1)}, u32[]{:S(2)}) %copy-start.3) | copy-done | bytes 524312
  4.4 0.0 copy-start.4
  4.4 0.9 %copy-done.4 = f32[2,256,128]{2,1,0:T(8,128)S(1)} copy-done((f32[2,256,128]{2,1,0:T(8,128)S(1)}, f32[2,256,128]{2,1,0:T(8,128)}, u32[]{:S(2)}) %copy-start.4) | copy-done | bytes 262168
  5.4 0.0 copy-start.5
  5.4 0.9 %copy-done.5 = bf16[128,512]{1,0:T(8,128)(2,1)S(1)} copy-done((bf16[128,512]{1,0:T(8,128)(2,1)S(1)}, bf16[128,512]{1,0:T(8,128)(2,1)}, u32[]{:S(2)}) %copy-start.5) | copy-done | bytes 131096
  6.3 0.0 copy-start.6
  6.3 0.9 %copy-done.6 = bf16[256,256]{1,0:T(8,128)(2,1)S(1)} copy-done((bf16[256,256]{1,0:T(8,128)(2,1)S(1)}, bf16[256,256]{1,0:T(8,128)(2,1)}, u32[]{:S(2)}) %copy-start.6) | copy-done | bytes 131096
  7.2 0.0 copy-start.7
  7.2 0.7 %copy-done.7 = f32[4,2,256]{2,1,0:T(2,128)S(1)} copy-done((f32[4,2,256]{2,1,0:T(2,128)S(1)}, f32[4,2,256]{2,1,0:T(2,128)}, u32[]{:S(2)}) %copy-start.7) | copy-done | bytes 8216
  7.9 48.6 %shard_map.100 = f32[256,256]{1,0:T(8,128)S(1)} custom-call(f32[256,4096]{1,0:T(8,128)} %t_hbm.1, f32[12,2,256,256]{3,2,1,0:T(8,128)} %k_hbm.1, bf16[2,512,512]{2,1,0:T(8,128)(2,1)S(1)} %copy-done, f32[4,2,256]{2,1,0:T(2,128)S(1)} %copy-done.7, bf16[256,256]{1,0:T(8,128)(2,1)S(1)} %copy-done.6, bf16[2,512,256]{2,1,0:T(8,128)(2,1)S(1)} %copy-done.3, ...), custom_call_target="tpu_custom_call" | custom-call | tf_op jit(solution)/shard_map/pallas_call | solution.py:284
  56.5 0.7 %copy.12 = f32[256,256]{1,0:T(8,128)} copy(f32[256,256]{1,0:T(8,128)S(1)} %shard_map.100) | data formatting | bytes 524288
Async XLA Ops:
  0.0 1.2 %copy-start = (bf16[2,512,512]{2,1,0:T(8,128)(2,1)S(1)}, bf16[2,512,512]{2,1,0:T(8,128)(2,1)}, u32[]{:S(2)}) copy-start(bf16[2,512,512]{2,1,0:T(8,128)(2,1)} %constant.16.clone.refs_0_) | copy-start | bytes 3145732
  1.2 1.1 %copy-start.1 = (bf16[2,256,768]{2,1,0:T(8,128)(2,1)S(1)}, bf16[2,256,768]{2,1,0:T(8,128)(2,1)}, u32[]{:S(2)}) copy-start(bf16[2,256,768]{2,1,0:T(8,128)(2,1)} %constant.22.clone.refs_6_) | copy-start | bytes 2359300
  2.4 1.0 %copy-start.2 = (bf16[2,256,512]{2,1,0:T(8,128)(2,1)S(1)}, bf16[2,256,512]{2,1,0:T(8,128)(2,1)}, u32[]{:S(2)}) copy-start(bf16[2,256,512]{2,1,0:T(8,128)(2,1)} %constant.23.clone.refs_7_) | copy-start | bytes 1572868
  3.4 1.0 %copy-start.3 = (bf16[2,512,256]{2,1,0:T(8,128)(2,1)S(1)}, bf16[2,512,256]{2,1,0:T(8,128)(2,1)}, u32[]{:S(2)}) copy-start(bf16[2,512,256]{2,1,0:T(8,128)(2,1)} %constant.19.clone.refs_3_) | copy-start | bytes 1572868
  4.4 0.9 %copy-start.4 = (f32[2,256,128]{2,1,0:T(8,128)S(1)}, f32[2,256,128]{2,1,0:T(8,128)}, u32[]{:S(2)}) copy-start(f32[2,256,128]{2,1,0:T(8,128)} %constant.20.clone.refs_4_) | copy-start | bytes 786436
  5.4 0.9 %copy-start.5 = (bf16[128,512]{1,0:T(8,128)(2,1)S(1)}, bf16[128,512]{1,0:T(8,128)(2,1)}, u32[]{:S(2)}) copy-start(bf16[128,512]{1,0:T(8,128)(2,1)} %constant.21.clone.refs_5_) | copy-start | bytes 393220
  6.3 0.9 %copy-start.6 = (bf16[256,256]{1,0:T(8,128)(2,1)S(1)}, bf16[256,256]{1,0:T(8,128)(2,1)}, u32[]{:S(2)}) copy-start(bf16[256,256]{1,0:T(8,128)(2,1)} %constant.18.clone.refs_2_) | copy-start | bytes 393220
  7.2 0.7 %copy-start.7 = (f32[4,2,256]{2,1,0:T(2,128)S(1)}, f32[4,2,256]{2,1,0:T(2,128)}, u32[]{:S(2)}) copy-start(f32[4,2,256]{2,1,0:T(2,128)} %constant.17.clone.refs_1_) | copy-start | bytes 24580

commit v2 on v1

--- a/solution.py
+++ b/solution.py
@@ -40,7 +40,7 @@
     turn = angle(starts, both, side)
     twiddle = np.stack([np.cos(turn), np.sin(turn)], axis=1).astype(np.float32)
     order = (both[:, None] == frequency[None, :]).astype(jnp.bfloat16)
-    x = angle(np.arange(rows), frequency, side).T
+    x = angle(np.arange(rows), frequency[: band // 2], side).T
     row = np.concatenate([np.cos(x), np.sin(x)], axis=0)
     lanes = -(-slabs // LANES) * LANES
     first = angle(np.arange(lanes) * rows, frequency, side).T
@@ -96,7 +96,7 @@
     scratch = refs[count + 1 :]
     t_ref, k_ref = scratch[:2]
     tab = dict(zip(NAMES, scratch[2 : 2 + count]))
-    (acc, sbuf, rbuf, fbuf, spec, lbuf, ibuf, load_sem, t_sem, ssem, rsem) = scratch[2 + count :]
+    (acc, sbuf, pbuf, csum, rbuf, fbuf, esend, epsum, erecv, spec, lbuf, ibuf, load_sem, t_sem, ssem, rsem) = scratch[2 + count :]
     me = lax.axis_index("slab")
     rows, side = t_ref.shape
     kernels, _, band, _ = k_ref.shape
@@ -105,12 +105,30 @@
     part = sbuf.shape[0] // slabs
     samples = ibuf.shape[1]
 
+    chips = slabs // 2
+    chip, core = me // 2, lax.rem(me, 2)
+    partner = me + 1 - 2 * core
+    low = band // 2
+
     def peer(k):
-        return lax.rem(me + k, slabs)
+        return 2 * lax.rem(chip + k, chips) + core
+
+    def place(of_chip, of_core):
+        return pl.ds(pl.multiple_of((of_core * chips + of_chip) * part, part), part)
+
+    def remote(src, dst, phase, index, to):
+        return pltpu.make_async_remote_copy(
+            src_ref=src,
+            dst_ref=dst,
+            send_sem=ssem.at[phase, index],
+            recv_sem=rsem.at[phase, index],
+            device_id={"slab": to},
+            device_id_type=MESH,
+        )
 
     barrier = pltpu.get_barrier_semaphore()
-    for k in range(1, slabs):
-        pl.semaphore_signal(barrier, inc=1, device_id={"slab": peer(k)}, device_id_type=MESH)
+    for to in [partner] + [peer(k) for k in range(1, chips)]:
+        pl.semaphore_signal(barrier, inc=1, device_id={"slab": to}, device_id_type=MESH)
 
     loads = {}
     for i, name in enumerate(NAMES):
@@ -164,63 +182,101 @@
     loads["order"].wait()
     loads["row"].wait()
     loads["phase"].wait()
-    ordered = []
-    for lanes in (slice(0, band), slice(band, 2 * band)):
-        ordered.append([dot(p, tab["order"][...]).astype(jnp.bfloat16) for p in split(acc[:, lanes])])
-    columns = [jnp.concatenate([ordered[0][i], ordered[1][i]], axis=1) for i in range(2)]
+    ordered = [
+        [dot(p, tab["order"][...]) for p in split(acc[:, lanes])]
+        for lanes in (slice(0, band), slice(band, 2 * band))
+    ]
+    columns = [
+        jnp.concatenate([ordered[0][i].astype(jnp.bfloat16), ordered[1][i].astype(jnp.bfloat16)], axis=1)
+        for i in range(2)
+    ]
     z = dot3((tab["row"][0], tab["row"][1]), columns)
-    re = z[:band, :band] - z[band:, band:]
-    im = -(z[:band, band:] + z[band:, :band])
+    zcc, zcs, zsc, zss = z[:low, :band], z[:low, band:], z[low:, :band], z[low:, band:]
     lane = lax.broadcasted_iota(jnp.int32, tab["phase"].shape[1:], 1)
     pc = jnp.sum(jnp.where(lane == me, tab["phase"][0], 0.0), axis=1, keepdims=True)
     ps = jnp.sum(jnp.where(lane == me, tab["phase"][1], 0.0), axis=1, keepdims=True)
-    sbuf[:band, :] = re * pc + im * ps
-    sbuf[band:, :] = im * pc - re * ps
-
-    pl.semaphore_wait(barrier, slabs - 1)
-    sends = []
-    for k in range(1, slabs):
-        to = peer(k)
-        sends.append(
-            pltpu.make_async_remote_copy(
-                src_ref=sbuf.at[pl.ds(pl.multiple_of(to * part, part), part)],
-                dst_ref=rbuf.at[k - 1],
-                send_sem=ssem.at[0, k - 1],
-                recv_sem=rsem.at[0, k - 1],
-                device_id={"slab": to},
-                device_id_type=MESH,
-            )
-        )
+    nc, ns = pc[:low], ps[:low]
+    re, im = zcc - zss, -(zcs + zsc)
+    re, im = re * nc + im * ns, im * nc - re * ns
+    sbuf[:low, :] = re[:, :low]
+    sbuf[low : 2 * low, :] = re[:, low:]
+    sbuf[2 * low : 3 * low, :] = im[:, :low]
+    sbuf[3 * low :, :] = im[:, low:]
+    esend[0:1, :band] = jnp.sum(ordered[0][0] + ordered[0][1], axis=0, keepdims=True)
+    esend[0:1, band : 2 * band] = -jnp.sum(ordered[1][0] + ordered[1][1], axis=0, keepdims=True)
+    re, im = (zcc + zss)[:, :low], (zcs - zsc)[:, :low]
+    re, im = re * nc + im * ns, im * nc - re * ns
+    esend[0:1, 2 * band : 2 * band + low] = re.T[0:1]
+    esend[0:1, 2 * band + low :] = im.T[0:1]
+
+    pl.semaphore_wait(barrier, chips)
+    length = chips * part
+    mine = pl.ds(pl.multiple_of(core * length, length), length)
+    theirs = pl.ds(pl.multiple_of((1 - core) * length, length), length)
+    pair = remote(sbuf.at[theirs], pbuf, 0, 0, partner)
+    epair = remote(esend, erecv.at[0], 1, 0, partner)
+    pair.start()
+    epair.start()
+    pair.wait_recv()
+    csum[...] = sbuf[mine, :] + pbuf[...]
+    epair.wait_recv()
+    epsum[...] = esend[...] + erecv[0]
+    sends, esends = [], []
+    for k in range(1, chips):
+        to = lax.rem(chip + k, chips)
+        piece = pl.ds(pl.multiple_of(to * part, part), part)
+        sends.append(remote(csum.at[piece], rbuf.at[k - 1], 0, k, peer(k)))
+        esends.append(remote(epsum, erecv.at[k], 1, k, peer(k)))
         sends[-1].start()
-    own = pl.ds(pl.multiple_of(me * part, part), part)
-    total = sbuf[own, :]
-    for k in range(1, slabs):
+        esends[-1].start()
+    total = csum[pl.ds(pl.multiple_of(chip * part, part), part), :]
+    for k in range(1, chips):
         sends[k - 1].wait_recv()
         total = total + rbuf[k - 1]
+    own = place(chip, core)
     fbuf[own, :] = total
-    shares = []
-    for k in range(1, slabs):
-        shares.append(
-            pltpu.make_async_remote_copy(
-                src_ref=fbuf.at[own],
-                dst_ref=fbuf.at[own],
-                send_sem=ssem.at[1, k - 1],
-                recv_sem=rsem.at[1, k - 1],
-                device_id={"slab": peer(k)},
-                device_id_type=MESH,
-            )
-        )
-        shares[-1].start()
-    for send in sends:
-        send.wait_send()
+    shares = [remote(fbuf.at[own], fbuf.at[own], 2, k, peer(k)) for k in range(1, chips)]
+    for share in shares:
+        share.start()
+    passed = [remote(fbuf.at[own], fbuf.at[own], 3, 0, partner)]
+    passed[0].start()
+    edge = epsum[...]
+    for k in range(1, chips):
+        esends[k - 1].wait_recv()
+        edge = edge + erecv[k]
     k_load.wait()
     for name in ("sample", "window", "spread"):
         loads[name].wait()
-    for share in shares:
-        share.wait_recv()
+    for k in range(1, chips):
+        shares[k - 1].wait_recv()
+        region = fbuf.at[place(lax.rem(chip - k + chips, chips), core)]
+        passed.append(remote(region, region, 3, k, partner))
+        passed[-1].start()
+    for p in passed:
+        p.wait_recv()
+
+    mre = jnp.concatenate([fbuf[:low, :], fbuf[low : 2 * low, :]], axis=1)
+    mim = jnp.concatenate([fbuf[2 * low : 3 * low, :], fbuf[3 * low :, :]], axis=1)
+    cells = [lax.broadcasted_iota(jnp.int32, (band, band), i) for i in range(2)]
+    mirror = (cells[0] + cells[1] == band).astype(jnp.float32).astype(jnp.bfloat16)
+    cells = [lax.broadcasted_iota(jnp.int32, (low, low), i) for i in range(2)]
+    flip = (cells[0] + cells[1] == low).astype(jnp.float32).astype(jnp.bfloat16)
+    turned = dot(jnp.concatenate([*split(mre), *split(mim)], axis=0), mirror)
+    first = lax.broadcasted_iota(jnp.int32, (low, band), 1) == 0
+    parts = []
+    for i in range(2):
+        both = turned[2 * i * low : (2 * i + 1) * low] + turned[(2 * i + 1) * low : (2 * i + 2) * low]
+        corner = edge[:, 2 * band + i * low : 2 * band + (i + 1) * low]
+        corner = jnp.broadcast_to(corner, (low, low)).T[:, 0:1]
+        parts += split(jnp.where(first, corner, both))
+    flipped = dot(flip, jnp.concatenate(parts, axis=1))
+    top = lax.broadcasted_iota(jnp.int32, (low, band), 0) == 0
+    fre = jnp.where(top, edge[:, :band], flipped[:, :band] + flipped[:, band : 2 * band])
+    fim = jnp.where(top, edge[:, band : 2 * band], -(flipped[:, 2 * band : 3 * band] + flipped[:, 3 * band :]))
 
     norm = 1.0 / (side * band)
-    re, im = fbuf[:band, :], fbuf[band:, :]
+    re = jnp.concatenate([mre, fre], axis=0)
+    im = jnp.concatenate([mim, fim], axis=0)
     spec[:band, :] = (re * pc - im * ps) * norm
     spec[band:, :] = (im * pc + re * ps) * norm
 
@@ -248,27 +304,24 @@
         blurred = blurred + binomial[v] * pltpu.roll(intensity, width - v, 1)
     ibuf[0] = blurred[:, :COLS]
 
-    rings = []
-    for k in range(1, slabs):
-        rings.append(
-            pltpu.make_async_remote_copy(
-                src_ref=ibuf.at[0],
-                dst_ref=ibuf.at[slabs - k],
-                send_sem=ssem.at[2, k - 1],
-                recv_sem=rsem.at[2, k - 1],
-                device_id={"slab": peer(k)},
-                device_id_type=MESH,
-            )
-        )
-        rings[-1].start()
-    for share in shares:
-        share.wait_send()
+    rings = [
+        remote(ibuf.at[0], ibuf.at[slabs - 2 * k], 4, k, peer(k)) for k in range(1, chips)
+    ]
     for ring in rings:
-        ring.wait_recv()
+        ring.start()
+    beside = [remote(ibuf.at[0], ibuf.at[lax.rem(slabs - 1 + 2 * core, slabs)], 5, 0, partner)]
+    beside[0].start()
+    for k in range(1, chips):
+        rings[k - 1].wait_recv()
+        slot = lax.rem(slabs - 2 * k - 1 + 2 * core + slabs, slabs)
+        beside.append(remote(ibuf.at[slabs - 2 * k], ibuf.at[slot], 5, k, partner))
+        beside[-1].start()
+    for b in beside:
+        b.wait_recv()
     gathered = split(ibuf[...].reshape(slabs * samples, COLS))
     out[...] = dot3((tab["spread"][0], tab["spread"][1]), gathered)
-    for ring in rings:
-        ring.wait_send()
+    for copy in [pair, epair] + sends + esends + shares + passed + rings + beside:
+        copy.wait_send()
 
 
 def local(transmission, kernel_spectra):
@@ -280,6 +333,7 @@
     arrays = [jnp.asarray(consts[name]) for name in NAMES]
     samples = rows * 2 * band // side
     part = 2 * band // slabs
+    chips, low = slabs // 2, band // 2
     any_spec = pl.BlockSpec(memory_space=pl.ANY)
     return pl.pallas_call(
         functools.partial(body, slabs, chunk),
@@ -291,19 +345,24 @@
             pltpu.VMEM(kernel_spectra.shape, jnp.float32),
             *[pltpu.VMEM(a.shape, a.dtype) for a in arrays],
             pltpu.VMEM((rows, 2 * band), jnp.float32),
-            pltpu.VMEM((2 * band, band), jnp.float32),
-            pltpu.VMEM((slabs - 1, part, band), jnp.float32),
-            pltpu.VMEM((2 * band, band), jnp.float32),
+            pltpu.VMEM((2 * band, low), jnp.float32),
+            pltpu.VMEM((chips * part, low), jnp.float32),
+            pltpu.VMEM((chips * part, low), jnp.float32),
+            pltpu.VMEM((chips - 1, part, low), jnp.float32),
+            pltpu.VMEM((2 * band, low), jnp.float32),
+            pltpu.VMEM((1, 3 * band), jnp.float32),
+            pltpu.VMEM((1, 3 * band), jnp.float32),
+            pltpu.VMEM((chips, 1, 3 * band), jnp.float32),
             pltpu.VMEM((2 * band, band), jnp.float32),
             pltpu.VMEM((kernels, 2 * samples, band), jnp.float32),
             pltpu.VMEM((slabs, samples, COLS), jnp.float32),
             pltpu.SemaphoreType.DMA((len(NAMES) + 1,)),
             pltpu.SemaphoreType.DMA((2 * (side // 2 // chunk),)),
-            pltpu.SemaphoreType.DMA((3, slabs - 1)),
-            pltpu.SemaphoreType.DMA((3, slabs - 1)),
+            pltpu.SemaphoreType.DMA((6, chips)),
+            pltpu.SemaphoreType.DMA((6, chips)),
         ],
         compiler_params=pltpu.CompilerParams(
-            collective_id=0, has_side_effects=True, vmem_limit_bytes=48 * 1024 * 1024
+            collective_id=0, has_side_effects=True, vmem_limit_bytes=67_043_328
         ),
     )(transmission, kernel_spectra, *arrays)
 

time: 57.6 us -> 36.9 us (0.64)
  the two profiles are of different devices: /device:TPU:13 before, /device:TPU:0 now
where the time goes in v2:
time: 36.9 us; the launch traced here: 36.7 us
  Pallas kernels  35 us (95%)
  local copies, waits for them, and re-layouts  1.67 us (5%)
    pallas_call x1, Pallas kernels, local(): pl.pallas_call(functools.partial(body, slabs, chunk), out_shape=jax.Shape...  35 us
    unnamed x1, local copies, waits for them, and re-layouts  1.67 us

profile of v2, /device:TPU:0, one launch (start us, length us, event | category | flops | bytes accessed | tf_op | source)
XLA Modules:
  0.0 36.7 jit_solution(1616037152552703662)
XLA Ops:
  0.0 35.0 %shard_map.100 = f32[256,256]{1,0:T(8,128)} custom-call(f32[256,4096]{1,0:T(8,128)} %t_hbm.1, f32[12,2,256,256]{3,2,1,0:T(8,128)} %k_hbm.1, bf16[2,512,512]{2,1,0:T(8,128)(2,1)} %constant.16.clone.refs_0_, f32[4,2,256]{2,1,0:T(2,128)} %constant.17.clone.refs_1_, bf16[256,256]{1,0:T(8,128)(2,1)} %constant.18.clone.refs_2_, ...), custom_call_target="tpu_custom_call" | custom-call | tf_op jit(solution)/shard_map/pallas_call | solution.py:338
  35.0 1.7 %copy.12 = f32[256,256]{1,0:T(8,128)} copy(f32[256,256]{1,0:T(8,128)} %shard_map.100) | data formatting | bytes 524288

commit v3 on v2

--- a/solution.py
+++ b/solution.py
@@ -151,9 +151,6 @@
         load.start()
     for name in ("order", "row", "phase"):
         loads[name].start()
-    k_load.start()
-    for name in ("sample", "window", "spread"):
-        loads[name].start()
 
     for c in range(steps):
         t_loads[2 * c].wait()
@@ -179,6 +176,9 @@
                 acc[:, near] += cosine * tc - sine * ts
                 acc[:, far] += sine * tc + cosine * ts
 
+    k_load.start()
+    for name in ("sample", "window", "spread"):
+        loads[name].start()
     loads["order"].wait()
     loads["row"].wait()
     loads["phase"].wait()
@@ -291,7 +291,7 @@
         lbuf[k] = wide[: 2 * samples] + wide[2 * samples :] + dot(tab["sample"][: 2 * samples, :], low)
         return carry
 
-    lax.fori_loop(0, kernels, one, 0)
+    lax.fori_loop(0, kernels, one, 0, unroll=True)
     left = split(lbuf[...].reshape(kernels * 2 * samples, band))
     field = dot3(left, (tab["window"][0], tab["window"][1]))
     width = field.shape[1] // 2

time: 36.9 us -> 34.6 us (0.938)
  Pallas kernels: 35 us -> 32.7 us
    pallas_call x1, Pallas kernels: 35 us -> 32.7 us  [local(): pl.pallas_call(functools.partial(body, slabs, chunk), out_shape=jax.Shape...]
where the time goes in v3:
time: 34.6 us; the launch traced here: 34.4 us
  Pallas kernels  32.7 us (95%)
  local copies, waits for them, and re-layouts  1.67 us (5%)
    pallas_call x1, Pallas kernels, local(): pl.pallas_call(functools.partial(body, slabs, chunk), out_shape=jax.Shape...  32.7 us
    unnamed x1, local copies, waits for them, and re-layouts  1.67 us

profile of v3, /device:TPU:0, one launch (start us, length us, event | category | flops | bytes accessed | tf_op | source)
XLA Modules:
  0.0 34.4 jit_solution(15528474772645952329)
XLA Ops:
  0.0 32.7 %shard_map.100 = f32[256,256]{1,0:T(8,128)} custom-call(f32[256,4096]{1,0:T(8,128)} %t_hbm.1, f32[12,2,256,256]{3,2,1,0:T(8,128)} %k_hbm.1, bf16[2,512,512]{2,1,0:T(8,128)(2,1)} %constant.16.clone.refs_0_, f32[4,2,256]{2,1,0:T(2,128)} %constant.17.clone.refs_1_, bf16[256,256]{1,0:T(8,128)(2,1)} %constant.18.clone.refs_2_, ...), custom_call_target="tpu_custom_call" | custom-call | tf_op jit(solution)/shard_map/pallas_call | solution.py:338
  32.8 1.7 %copy.12 = f32[256,256]{1,0:T(8,128)} copy(f32[256,256]{1,0:T(8,128)} %shard_map.100) | data formatting | bytes 524288
